TPU v7x, 32 devices: a whole 2x2x4 slice. The times are simulated.
32 devices in a mesh: cpi: 2 (over y), rng: 4 (over z), bin: 2 (over x), chn: 2 (over core).
Axes of the slice: x: 2, y: 2, z: 4, core: 2. Of those that a mesh axis runs over, the one named last changes fastest.
Arguments:
- samples: bfloat16 [16, 8192, 384], P(('cpi', 'bin'), 'rng', 'chn'), parts along dimension 0, may hold values from -16 to 16
- train_mask: int32 [16, 8192], P(('cpi', 'bin'), 'rng'), parts along dimension 0, may hold values 0 or 1
- angles: int32 [32], P('cpi'), parts along dimension 0, may hold values from 0 to 127
Outputs:
- amf_stat: float32 [16, 16, 8192], P(('cpi', 'bin'), None, ('rng', 'chn')), parts along dimension 0
- gate_power: float32 [16, 8192], P(('cpi', 'bin'), ('rng', 'chn')), parts along dimension 0
There are 2 independent parts, one for each index of `cpi`. A program takes and returns all parts, laid end to end along the dimension named above; each array names one. Nothing has to cross between parts.
All inputs are finite; a program needn't handle non-finite values. No bound on the sum of `train_mask` on one device may be relied on, other than what follows from the above.
Results may differ from a plain program's by a relative error of at most 0.0004.
Values may be sent and summed in bfloat16 or wider, within the bound.
A program may use at most 128 MiB of HBM per device.

v0:
```python
import jax
import jax.numpy as jnp
from jax import lax
from jax.sharding import PartitionSpec as P

ANGLES = 128


LOAD = 0.1


def steering(angles, channels):
    elements = channels // 2
    phase = jnp.pi * jnp.sin(jnp.pi * (angles.astype(jnp.float32) / ANGLES - 0.5))
    element_pos = jnp.arange(elements).astype(jnp.float32)
    turns = element_pos[:, None] * phase[None, :]
    return jnp.concatenate([jnp.cos(turns), jnp.sin(turns)], axis=0)


def whiten_and_test(gram_sum, counts, tested, angles):
    channels = tested.shape[2]
    identity = jnp.eye(channels, dtype=jnp.float32)
    covariance = gram_sum / jnp.maximum(counts, 1.0)[:, None, None] + LOAD * identity[None]
    factor = jnp.linalg.cholesky(covariance)
    steer = steering(angles, channels)
    steer_batch = jnp.broadcast_to(steer, (factor.shape[0],) + steer.shape)
    white_steer = jax.scipy.linalg.solve_triangular(factor, steer_batch, lower=True)
    steer_power = jnp.sum(white_steer * white_steer, axis=1)
    filters = jax.scipy.linalg.solve_triangular(factor, white_steer, lower=True, trans=1)
    columns = jnp.swapaxes(tested.astype(jnp.float32), 1, 2)
    projected = jnp.einsum("bck,bcg->bkg", filters, columns, precision=lax.Precision.HIGHEST)
    amf_stat = projected * projected / steer_power[:, :, None]
    white_gates = jax.scipy.linalg.solve_triangular(factor, columns, lower=True)
    gate_power = jnp.sum(white_gates * white_gates, axis=1) / channels
    return (amf_stat, gate_power)


def body(samples, train_mask, angles):
    cores = lax.axis_size("chn")
    core_index = lax.axis_index("chn")
    half_gates = samples.shape[1] // cores
    complete = lax.all_gather(samples, "chn", axis=2, tiled=True)
    weights = train_mask.astype(jnp.bfloat16)
    masked = samples * weights[:, :, None]
    row_part = jnp.einsum("bgc,bgd->bcd", masked, complete, preferred_element_type=jnp.float32)
    count_part = jnp.sum(train_mask.astype(jnp.float32), axis=1)
    row_sum, counts = lax.psum((row_part, count_part), "rng")
    gram_sum = lax.all_gather(row_sum, "chn", axis=1, tiled=True)
    tested = lax.dynamic_slice_in_dim(complete, core_index * half_gates, half_gates, 1)
    return whiten_and_test(gram_sum, counts, tested, angles)


def solution(mesh):
    placed = (P(("cpi", "bin"), "rng", "chn"), P(("cpi", "bin"), "rng"), P("cpi"))
    return jax.shard_map(
        body,
        mesh=mesh,
        in_specs=placed,
        out_specs=(P(("cpi", "bin"), None, ("rng", "chn")), P(("cpi", "bin"), ("rng", "chn"))),
        check_vma=False,
    )
```

profile of v0, /device:TPU:24, one launch (start us, length us, event | category | flops | bytes accessed | tf_op | source)
XLA Modules:
  0.0 508.1 jit_solution(7026084522248947398)
XLA Ops:
  8.9 18.7 %all-gather.3.cloned.1.call-done = bf16[4,2048,384]{1,2,0:T(8,128)(2,1)} async-done(((bf16[4,2048,192]{1,2,0:T(8,128)(2,1)}), bf16[4,2048,384]{1,2,0:T(8,128)(2,1)}) %all-gather.3.cloned.1.call-update) | async-done | bytes 6291472 | tf_op jit(solution)/shard_map/all_gather | solution.py:42
  27.6 6.0 %fusion.5 = f32[4,192,384]{2,1,0:T(8,128)} fusion(bf16[4,2048,384]{1,2,0:T(8,128)(2,1)} %all-gather.3.cloned.1.call-done, bf16[4,2048,192]{1,2,0:T(8,128)(2,1)S(1)} %copy-done.2, bf16[4,2048]{1,0:T(4,128)(2,1)S(1)} %convert_element_type.19), kind=kOutput, calls=%fused_computation.8 | convolution fusion | flops 1209532416 | bytes 10633216 | tf_op jit(solution)/shard_map/bgc,bgd->bcd/dot_general | solution.py:45
  33.7 55.5 %all-reduce.3.cloned.1.call-done = f32[4,192,384]{2,1,0:T(8,128)} async-done(((f32[4,192,384]{2,1,0:T(8,128)}), f32[4,192,384]{2,1,0:T(8,128)}) %all-reduce.3.cloned.1.call-update) | async-done | bytes 1179664 | tf_op jit(solution)/shard_map/psum | solution.py:47
  89.2 3.0 copy.38
  92.4 9.0 %psum.15 = f32[4]{0:T(128)S(1)} all-reduce(f32[4]{0:T(128)S(1)} %convert_reduce_fusion), channel_id=1, replica_groups=mesh['cpi'=2,'rng'=4,'bin'=2,'chn'=2] {'rng'}, use_global_device_ids=true, to_apply=%region_2.0 | all-reduce | flops 4 | bytes 32 | tf_op jit(solution)/shard_map/psum | solution.py:47
  103.5 6.5 %fusion.60 = (f32[4,384,1024]{2,1,0:T(8,128)}, bf16[4,384,1024]{2,1,0:T(8,128)(2,1)}) fusion(bf16[4,2048,384]{1,2,0:T(8,128)(2,1)} %all-gather.3.cloned.1.call-done, s32[]{:T(128)S(6)} %select_n.8), kind=kLoop, calls=%fused_computation.101 | loop fusion | flops 1572864 | bytes 12582916 | tf_op jit(solution)/shard_map/transpose | solution.py:30
  110.0 2.8 copy.39
  114.5 3.1 copy.40
  117.5 2.1 fusion.9
  121.0 46.9 %custom-call.32 = f32[4,128,128]{2,1,0:T(8,128)S(1)} custom-call(f32[4,128,128]{2,1,0:T(8,128)S(1)} %cholesky.198), custom_call_target="Cholesky" | custom-call | tf_op jit(solution)/shard_map/jit(cholesky)/cholesky | solution.py:24
  168.0 39.3 %custom-call.33 = f32[4,1,128,128]{2,3,1,0:T(8,128)S(1)} custom-call(f32[4,1,128,128]{3,2,1,0:T(8,128)S(1)} %select_bitcast_fusion.1), custom_call_target="InvertDiagBlocksLowerTriangular" | custom-call | tf_op jit(solution)/shard_map/jit(cholesky)/cholesky | solution.py:24
  211.5 47.8 %custom-call.34 = f32[4,128,128]{2,1,0:T(8,128)S(1)} custom-call(f32[4,128,128]{2,1,0:T(8,128)} %cholesky.202), custom_call_target="Cholesky" | custom-call | tf_op jit(solution)/shard_map/jit(cholesky)/cholesky | solution.py:24
  260.8 40.7 %custom-call.35 = f32[4,1,128,128]{2,3,1,0:T(8,128)} custom-call(f32[4,1,128,128]{3,2,1,0:T(8,128)} %get-tuple-element.26), custom_call_target="InvertDiagBlocksLowerTriangular" | custom-call | tf_op jit(solution)/shard_map/jit(cholesky)/cholesky | solution.py:24
  304.5 46.9 %custom-call.36 = f32[4,128,128]{2,1,0:T(8,128)S(1)} custom-call(f32[4,128,128]{2,1,0:T(8,128)S(1)} %convolution_subtract_fusion.1), custom_call_target="Cholesky" | custom-call | tf_op jit(solution)/shard_map/jit(cholesky)/cholesky | solution.py:24
  353.6 2.0 select_select_fusion
  355.7 8.2 %while.1 = (s32[]{:T(128)}, f32[4,384,384]{2,1,0:T(8,128)S(1)}, s32[3,2]{0,1:T(2,128)S(1)}, f32[3,4,128,128]{3,2,0,1:T(8,128)}, s32[]{:T(128)}) while((s32[]{:T(128)}, f32[4,384,384]{2,1,0:T(8,128)S(1)}, s32[3,2]{0,1:T(2,128)S(1)}, f32[3,4,128,128]{3,2,0,1:T(8,128)}, s32[]{:T(128)}) %tuple.33), condition=%wide.while_cond, body=%wide.while_body.sunk | while | flops 2 | bytes 525421 | solution.py:29
  356.3 2.2 bitcast_dynamic-update-slice_fusion.2
  359.0 2.2 bitcast_dynamic-update-slice_fusion.2
  361.8 2.1 bitcast_dynamic-update-slice_fusion.2
  363.9 118.9 %custom-call.37 = f32[4,3,128,128]{2,3,1,0:T(8,128)S(1)} custom-call(f32[4,3,128,128]{3,2,1,0:T(8,128)} %bitcast.65), custom_call_target="InvertDiagBlocksLowerTriangular" | custom-call | tf_op jit(solution)/shard_map/jit(_solve_triangular)/vmap()/triangular_solve | solution.py:29
  487.4 2.4 fusion.19
  491.8 2.0 fusion.11
  493.8 2.4 fusion.1
  499.3 2.0 fusion.16
  (86 shorter events, 29.1 us)
Async XLA Ops:
  7.2 20.4 %copy-start.2 = (bf16[4,2048,192]{1,2,0:T(8,128)(2,1)S(1)}, bf16[4,2048,192]{1,2,0:T(8,128)(2,1)}, u32[]{:S(2)}) copy-start(bf16[4,2048,192]{1,2,0:T(8,128)(2,1)} %param.3) | copy-start | bytes 9437188
  7.2 20.4 %all-gather.3.cloned.1.call-start = ((), (), s32[]{:S(2)}) async-start(), calls=%async_computation | async-start | bytes 9437184 | tf_op jit(solution)/shard_map/all_gather | solution.py:42
  7.9 81.3 %all-reduce.3.cloned.1.call-start = ((), (), s32[]{:S(2)}) async-start(), calls=%async_computation.1 | async-start | bytes 2359296 | tf_op jit(solution)/shard_map/psum | solution.py:47
  33.6 58.7 %copy-start.4 = (s32[4,2048]{1,0:T(4,128)S(1)}, s32[4,2048]{1,0:T(4,128)}, u32[]{:S(2)}) copy-start(s32[4,2048]{1,0:T(4,128)} %param.4) | copy-start | bytes 98308
  33.6 69.0 %copy-start.8 = (s32[16]{0:T(128)S(1)}, s32[16]{0:T(128)}, u32[]{:S(2)}) copy-start(s32[16]{0:T(128)} %param.5) | copy-start | bytes 196
  33.6 76.4 %all-gather.5.cloned.1.call-start = ((), (), s32[]{:S(2)}) async-start(), calls=%async_computation.2 | async-start | bytes 3538944 | tf_op jit(solution)/shard_map/all_gather | solution.py:48
  101.9 66.0 %copy-start.3 = (pred[128,128]{1,0:T(8,128)(4,1)}, pred[128,128]{1,0:T(8,128)(4,1)S(1)}, u32[]{:S(2)}) copy-start(pred[128,128]{1,0:T(8,128)(4,1)S(1)} %iota_compare_fusion.2) | copy-start | bytes 49156
  119.6 1.4 copy-start.1
  352.2 1.4 copy-start
  353.6 2.0 copy-start.9
  355.6 127.2 %copy-start.6 = (f32[128,16]{0,1:T(8,128)S(1)}, f32[128,16]{0,1:T(8,128)}, u32[]{:S(2)}) copy-start(f32[128,16]{0,1:T(8,128)} %get-tuple-element.30) | copy-start | bytes 24580
  355.6 127.5 %copy-start.7 = (f32[128,16]{0,1:T(8,128)S(1)}, f32[128,16]{0,1:T(8,128)}, u32[]{:S(2)}) copy-start(f32[128,16]{0,1:T(8,128)} %get-tuple-element.29) | copy-start | bytes 24580
  355.7 128.4 %copy-start.5 = (f32[128,16]{0,1:T(8,128)S(1)}, f32[128,16]{0,1:T(8,128)}, u32[]{:S(2)}) copy-start(f32[128,16]{0,1:T(8,128)} %get-tuple-element.28) | copy-start | bytes 24580
  483.2 8.6 %slice-start = ((s8[6291456]{0:T(1024)(128)(4,1)}), s8[4194304]{0:T(1024)(128)(4,1)S(1)}, s32[]{:S(2)}) async-start(s8[6291456]{0:T(1024)(128)(4,1)} %bitcast.61), calls=%async_computation.3 | async-start | bytes 8388608
  487.4 4.4 slice-start.1
  493.8 5.5 %slice-start.2 = ((s8[6291456]{0:T(1024)(128)(4,1)}), s8[4194304]{0:T(1024)(128)(4,1)S(1)}, s32[]{:S(2)}) async-start(s8[6291456]{0:T(1024)(128)(4,1)} %bitcast.63), calls=%async_computation.5 | async-start | bytes 8388608
  496.2 3.1 slice-start.3
Sparse Core Ops, SparseCore 0:
  9.5 17.9 all-gather.2
  33.7 55.3 all-reduce.2
  92.4 12.1 all-gather.4
where the time goes:
time: 517 us; the launch traced here: 508 us
  other arithmetic  360 us (70%)
  waiting for transfers between devices  74.9 us (14%)
  matrix products  29.4 us (6%)
  local copies, waits for them, and re-layouts  20.6 us (4%)
  between operations  14.3 us (3%)
  blocking collectives  9.01 us (2%)
    another operation x13, other arithmetic, whiten_and_test(): factor = jnp.linalg.cholesky(covariance)  225 us
    another operation x4, other arithmetic, whiten_and_test(): jax.scipy.linalg.solve_triangular(factor, white_steer, lower=True, trans=1)  121 us
    psum x1, waiting for transfers between devices, body(): row_sum, counts = lax.psum((row_part, count_part), 'rng')  55.5 us
    all_gather x1, waiting for transfers between devices, body(): complete = lax.all_gather(samples, 'chn', axis=2, tiled=True)  18.7 us
    another operation x5, matrix products, whiten_and_test(): white_gates = jax.scipy.linalg.solve_triangular(factor, columns, lower=True)  10.7 us
  transfers between devices with their start and end apart: 3, of which 2 were waited for; matrix products, arithmetic and copies ran while one was open for 2% of the time, Pallas kernels for 0%

commit v1 on v0

--- a/solution.py
+++ b/solution.py
@@ -1,12 +1,17 @@
+import functools
+
 import jax
 import jax.numpy as jnp
 from jax import lax
+from jax.experimental import pallas as pl
+from jax.experimental.pallas import tpu as pltpu
 from jax.sharding import PartitionSpec as P
 
 ANGLES = 128
-
-
 LOAD = 0.1
+T = 128
+MESH = pl.DeviceIdType.MESH
+HIGH = lax.Precision.HIGHEST
 
 
 def steering(angles, channels):
@@ -35,7 +40,7 @@
     return (amf_stat, gate_power)
 
 
-def body(samples, train_mask, angles):
+def plain_body(samples, train_mask, angles):
     cores = lax.axis_size("chn")
     core_index = lax.axis_index("chn")
     half_gates = samples.shape[1] // cores
@@ -50,8 +55,231 @@
     return whiten_and_test(gram_sum, counts, tested, angles)
 
 
+def invert_tile(a):
+    n = a.shape[0]
+    sub = lax.broadcasted_iota(jnp.int32, (8, n), 0)
+    lane = lax.broadcasted_iota(jnp.int32, (8, n), 1)
+    lane_all = lax.broadcasted_iota(jnp.int32, (n, n), 1)
+    for g in range(0, n, 8):
+        slab = a[g:g + 8, :]
+        cols = [jnp.broadcast_to(slab[:, g + j:g + j + 1], (8, n)) for j in range(8)]
+        inside = (lane >= g) & (lane < g + 8)
+        slab = jnp.where(inside, jnp.where(lane - g == sub, 1.0, 0.0), slab)
+        for k in range(8):
+            scale = 1.0 / cols[k][k:k + 1, :]
+            row = slab[k:k + 1, :] * scale
+            slab = jnp.where(sub == k, row, slab - cols[k] * row)
+            for j in range(k + 1, 8):
+                crow = cols[j][k:k + 1, :] * scale
+                cols[j] = jnp.where(sub == k, crow, cols[j] - cols[k] * crow)
+        rest = jnp.where((lane_all >= g) & (lane_all < g + 8), 0.0, a)
+        for j in range(8):
+            rest = rest - a[:, g + j:g + j + 1] * slab[j:j + 1, :]
+        pieces = [slab]
+        if g:
+            pieces = [rest[:g, :]] + pieces
+        if g + 8 < n:
+            pieces = pieces + [rest[g + 8:, :]]
+        a = jnp.concatenate(pieces, axis=0)
+    return a
+
+
+def dot(a, b, precision=None):
+    return jnp.dot(a, b, precision=precision, preferred_element_type=jnp.float32)
+
+
+def split3(a):
+    hi = a.astype(jnp.bfloat16)
+    left = a - hi.astype(jnp.float32)
+    mid = left.astype(jnp.bfloat16)
+    lo = (left - mid.astype(jnp.float32)).astype(jnp.bfloat16)
+    return hi, mid, lo
+
+
+def kernel(n, lower, x_hbm, mask_ref, steer_ref, amf_ref, pow_ref,
+           own, got, xt, gram, gram_rx, part, rs_rx, red, red_rx, mat, inv, ag_rx, fwd_rx, full,
+           lsem, xs, xr, gs, gr, rss, rsr, ds, dr, ags, agr, fs, fr):
+    r = lax.axis_index("rng")
+    c = lax.axis_index("chn")
+    other = 1 - c
+    bins, half, width = own.shape
+    chans = 2 * width
+    nb = chans // T
+    share = len(lower) // 2
+    rows = share * T
+
+    barrier = pltpu.get_barrier_semaphore()
+    pl.semaphore_signal(barrier, inc=1, device_id={"chn": other}, device_id_type=MESH)
+    for d in range(1, n):
+        pl.semaphore_signal(barrier, inc=1, device_id={"rng": lax.rem(r + d, n)}, device_id_type=MESH)
+
+    order = [lax.rem(r + d, n) for d in range(1, n)] + [r]
+    loads = []
+    for i, b in enumerate(order):
+        cp = pltpu.make_async_copy(x_hbm.at[b, pl.ds(pl.multiple_of(c * half, T), half), :], own.at[b], lsem.at[i])
+        cp.start()
+        loads.append(cp)
+    pl.semaphore_wait(barrier, n)
+
+    def remote(src, dst, send, recv, where):
+        cp = pltpu.make_async_remote_copy(src_ref=src, dst_ref=dst, send_sem=send, recv_sem=recv,
+                                          device_id=where, device_id_type=MESH)
+        cp.start()
+        return cp
+
+    swaps = [remote(x_hbm.at[b, pl.ds(pl.multiple_of(other * half, T), half), :], got.at[b],
+                    xs.at[i], xr.at[i], {"chn": other}) for i, b in enumerate(order)]
+
+    sends = []
+
+    def reduce_pair(i, b):
+        swap = gsw[i]
+        swap.wait()
+        for s in range(share):
+            part[b, s * T:(s + 1) * T, :] = gram[b, c * share + s] + gram_rx[b, s]
+        count = jnp.sum(mask_ref[b].astype(jnp.float32))
+        part[b, rows:rows + 8, :] = jnp.full((8, T), count, jnp.float32)
+        if i < n - 1:
+            sends.append(remote(part.at[b], rs_rx.at[i], rss.at[i], rsr.at[i], {"rng": b}))
+
+    gsw = []
+    for i, b in enumerate(order):
+        loads[i].wait()
+        swaps[i].wait()
+        mine, theirs = own[b], got[b]
+        first = c == 0
+        xt[b, :width, :] = jnp.where(first, mine, theirs).T
+        xt[b, width:, :] = jnp.where(first, theirs, mine).T
+        mask = mask_ref[b, :, pl.ds(pl.multiple_of(c * half, T), half)].astype(jnp.bfloat16)
+        xb = xt[b]
+        g = lax.dot_general(xb * mask, xb, (((1,), (1,)), ((), ())), preferred_element_type=jnp.float32)
+        for s, (p, q) in enumerate(lower):
+            gram[b, s] = g[p * T:(p + 1) * T, q * T:(q + 1) * T]
+        gsw.append(remote(gram.at[b, pl.ds(other * share, share)], gram_rx.at[b], gs.at[i], gr.at[i], {"chn": other}))
+        if i:
+            reduce_pair(i - 1, order[i - 1])
+    reduce_pair(n - 1, r)
+
+    total = part[r]
+    for cp in sends:
+        cp.wait()
+    for d in range(n - 1):
+        total = total + rs_rx[d]
+    red[...] = total
+    cp = remote(red, red_rx, ds, dr, {"chn": other})
+    scale = jnp.maximum(total[rows:rows + 1, :], 1.0)
+    cp.wait()
+    diag = jnp.where(lax.broadcasted_iota(jnp.int32, (T, T), 0) == lax.broadcasted_iota(jnp.int32, (T, T), 1), LOAD, 0.0)
+    for s, (p, q) in enumerate(lower):
+        lo = (s % share) * T
+        a, b = red[lo:lo + T, :], red_rx[lo:lo + T, :]
+        block = jnp.where(c == s // share, a, b) / scale
+        if p == q:
+            mat[p, p] = block + diag
+        else:
+            mat[p, q] = block
+            mat[q, p] = block.T
+
+    @pl.loop(0, nb)
+    def _(p):
+        tile = invert_tile(mat[p, p])
+        others = [lax.rem(p + d, nb) for d in range(1, nb)]
+        cross = [dot(tile, mat[p, j], HIGH) for j in others]
+        for i in others:
+            col = mat[i, p]
+            for j, e in zip(others, cross):
+                mat[i, j] = mat[i, j] - dot(col, e, HIGH)
+            mat[i, p] = -dot(col, tile, HIGH)
+        mat[p, p] = tile
+        for j, e in zip(others, cross):
+            mat[p, j] = e
+
+    for s, (p, q) in enumerate(lower):
+        inv[s] = mat[p, q]
+    gathers = [remote(inv.at[pl.ds(c * share, share)], ag_rx.at[d - 1], ags.at[d - 1], agr.at[d - 1],
+                      {"rng": lax.rem(r + d, n)}) for d in range(1, n)]
+    steer = steer_ref[...]
+    k = steer.shape[0]
+
+    def finish(b, blocks):
+        for (p, q), block in zip(lower, blocks):
+            full[p * T:(p + 1) * T, q * T:(q + 1) * T] = block
+            if p != q:
+                full[q * T:(q + 1) * T, p * T:(p + 1) * T] = block.T
+        s = full[...]
+        f = dot(steer, s, HIGH)
+        power = jnp.sum(f * steer, axis=1, keepdims=True)
+        xb = xt[b]
+        y = sum(dot(m, xb) for m in split3(s))
+        pow_ref[b] = jnp.sum(y * xb.astype(jnp.float32), axis=0, keepdims=True) / chans
+        z = sum(dot(m, xb) for m in split3(f))
+        amf_ref[b] = z * z / power
+
+    finish(r, [inv[s] for s in range(len(lower))])
+    forwards = []
+    for d in range(1, n):
+        gathers[d - 1].wait()
+        forwards.append(remote(ag_rx.at[d - 1], fwd_rx.at[d - 1], fs.at[d - 1], fr.at[d - 1], {"chn": other}))
+    for d in range(1, n):
+        forwards[d - 1].wait()
+        blocks = [jnp.where(c == s // share, ag_rx[d - 1, s % share], fwd_rx[d - 1, s % share])
+                  for s in range(len(lower))]
+        finish(lax.rem(r - d + n, n), blocks)
+
+
+def fused_body(samples, train_mask, angles):
+    bins, gates, width = samples.shape
+    n = lax.axis_size("rng")
+    half, chans = gates // 2, 2 * width
+    nb = chans // T
+    lower = [(i, j) for i in range(nb) for j in range(i + 1)]
+    share = len(lower) // 2
+    steer = steering(angles, chans).T
+    f32, bf16 = jnp.float32, jnp.bfloat16
+    sem = pltpu.SemaphoreType.DMA
+    vmem = pl.BlockSpec(memory_space=pltpu.VMEM)
+    rows = share * T + 8
+    amf, power = pl.pallas_call(
+        functools.partial(kernel, n, lower),
+        name="amf",
+        out_shape=(jax.ShapeDtypeStruct((bins, steer.shape[0], half), f32),
+                   jax.ShapeDtypeStruct((bins, 1, half), f32)),
+        in_specs=[pl.BlockSpec(memory_space=pl.ANY), vmem, vmem],
+        out_specs=(vmem, vmem),
+        scratch_shapes=[
+            pltpu.VMEM((bins, half, width), bf16),
+            pltpu.VMEM((bins, half, width), bf16),
+            pltpu.VMEM((bins, chans, half), bf16),
+            pltpu.VMEM((bins, len(lower), T, T), f32),
+            pltpu.VMEM((bins, share, T, T), f32),
+            pltpu.VMEM((bins, rows, T), f32),
+            pltpu.VMEM((n - 1, rows, T), f32),
+            pltpu.VMEM((rows, T), f32),
+            pltpu.VMEM((rows, T), f32),
+            pltpu.VMEM((nb, nb, T, T), f32),
+            pltpu.VMEM((len(lower), T, T), f32),
+            pltpu.VMEM((n - 1, share, T, T), f32),
+            pltpu.VMEM((n - 1, share, T, T), f32),
+            pltpu.VMEM((chans, chans), f32),
+            sem((n,)), sem((n,)), sem((n,)), sem((n,)), sem((n,)),
+            sem((n - 1,)), sem((n - 1,)), sem, sem,
+            sem((n - 1,)), sem((n - 1,)), sem((n - 1,)), sem((n - 1,)),
+        ],
+        compiler_params=pltpu.CompilerParams(collective_id=0, has_side_effects=True, vmem_limit_bytes=56 * 2**20),
+    )(samples, train_mask[:, None, :], steer)
+    return amf, power[:, 0, :]
+
+
 def solution(mesh):
     placed = (P(("cpi", "bin"), "rng", "chn"), P(("cpi", "bin"), "rng"), P("cpi"))
+
+    def body(samples, train_mask, angles):
+        bins, gates, width = samples.shape
+        nb = 2 * width // T
+        fits = (mesh.shape["chn"] == 2 and mesh.shape["rng"] == bins and bins > 1 and (2 * width) % T == 0
+                and gates % (2 * T) == 0 and nb * (nb + 1) // 2 % 2 == 0)
+        return (fused_body if fits else plain_body)(samples, train_mask, angles)
+
     return jax.shard_map(
         body,
         mesh=mesh,

time: 517 us -> 80.6 us (0.16); the launches traced: 508 us -> 80.1 us
  other arithmetic: 360 us -> 1.53 us
  waiting for transfers between devices: 74.9 us -> 0 us
  Pallas kernels: 0 us -> 67.6 us
  matrix products: 29.4 us -> 0 us
  between operations: 14.3 us -> 0.65 us
  local copies, waits for them, and re-layouts: 20.6 us -> 10.4 us
  blocking collectives: 9.01 us -> 0 us
    another operation x18 -> x0, other arithmetic: 347 us -> none  [the longest x13 225 us: whiten_and_test(): factor = jnp.linalg.cholesky(covariance)]
    pallas_call x0 -> x1, Pallas kernels: none -> 67.6 us  [fused_body(): pl.pallas_call(functools.partial(kernel, n, lower), name='amf', out_shape...]
    psum x1 -> x0, waiting for transfers between devices: 55.5 us -> none  [body(): row_sum, counts = lax.psum((row_part, count_part), 'rng')]
    another operation x19 -> x0, matrix products: 21.4 us -> none  [the longest x5 10.7 us: whiten_and_test(): white_gates = jax.scipy.linalg.solve_triangular(factor, columns, lower=True)]
    all_gather x2 -> x0, waiting for transfers between devices: 18.7 us -> none  [the longest x1 18.7 us: body(): complete = lax.all_gather(samples, 'chn', axis=2, tiled=True)]
    another operation x13 -> x0, local copies, waits for them, and re-layouts: 9.13 us -> none
    psum x1 -> x0, blocking collectives: 9.01 us -> none  [body(): row_sum, counts = lax.psum((row_part, count_part), 'rng')]
    dot_general x2 -> x0, matrix products: 8.07 us -> none  [the longest x1 6.03 us: body(): jnp.einsum('bgc,bgd->bcd', masked, complete, preferred_element_type=jnp.f...]
  transfers between devices with their start and end apart: 3 -> 0, of which waited for: 2 -> 0; matrix products, arithmetic and copies ran while one was open for 2% -> 0% of each run, Pallas kernels for 0% -> 0%
where the time goes in v1:
time: 80.6 us; the launch traced here: 80.1 us
  Pallas kernels  67.6 us (84%)
  local copies, waits for them, and re-layouts  10.4 us (13%)
  other arithmetic  1.53 us (2%)
    pallas_call x1, Pallas kernels, fused_body(): pl.pallas_call(functools.partial(kernel, n, lower), name='amf', out_shape...  67.6 us
    unnamed x3, local copies, waits for them, and re-layouts  8.98 us

profile of v1, /device:TPU:24, one launch (start us, length us, event | category | flops | bytes accessed | tf_op | source)
XLA Modules:
  0.0 80.1 jit_solution(3244348660883591430)
XLA Ops:
  0.6 0.7 sine_multiply_fusion
  1.3 0.1 multiply_cosine_fusion
  1.5 0.7 maximum_bitcast_fusion.steer_ref
  2.2 1.4 %broadcast_in_dim.2.mask_ref = s32[4,1,2048]{2,1,0:T(1,128)} reshape(s32[4,2048]{1,0:T(4,128)} %param.4) | data formatting | bytes 65536 | tf_op jit(solution)/shard_map/broadcast_in_dim | solution.py:269
  3.6 6.0 %copy.5.x_hbm = bf16[4,2048,192]{2,1,0:T(8,128)(2,1)} copy(bf16[4,2048,192]{1,2,0:T(8,128)(2,1)} %param.3) | data formatting | bytes 6291456 | tf_op args[0]
  9.5 67.6 %amf.1 = (f32[4,16,1024]{2,1,0:T(8,128)}, f32[4,1,1024]{2,1,0:T(1,128)}) custom-call(bf16[4,2048,192]{2,1,0:T(8,128)(2,1)} %copy.5.x_hbm, s32[4,1,2048]{2,1,0:T(1,128)} %broadcast_in_dim.2.mask_ref, f32[16,384]{1,0:T(8,128)} %maximum_bitcast_fusion.steer_ref), custom_call_target="tpu_custom_call" | custom-call | tf_op jit(solution)/shard_map/amf/pallas_call | solution.py:242
  77.1 1.3 %copy.8 = f32[4,1,1024]{2,0,1:T(4,128)} copy(f32[4,1,1024]{2,1,0:T(1,128)} %get-tuple-element.5) | data formatting | bytes 32768
  78.4 1.7 %copy.10 = f32[4,16,1024]{2,1,0:T(8,128)} copy(f32[4,16,1024]{2,1,0:T(8,128)} %get-tuple-element.10) | data formatting | bytes 524288
  (1 shorter events, 0.0 us)

commit v2 on v1

--- a/solution.py
+++ b/solution.py
@@ -97,13 +97,14 @@
 
 
 def kernel(n, lower, x_hbm, mask_ref, steer_ref, amf_ref, pow_ref,
-           own, got, xt, gram, gram_rx, part, rs_rx, red, red_rx, mat, inv, ag_rx, fwd_rx, full,
+           xt, gram, gram_rx, part, rs_rx, red, red_rx, mat, inv, ag_rx, fwd_rx, full,
            lsem, xs, xr, gs, gr, rss, rsr, ds, dr, ags, agr, fs, fr):
     r = lax.axis_index("rng")
     c = lax.axis_index("chn")
     other = 1 - c
-    bins, half, width = own.shape
-    chans = 2 * width
+    bins, chans, half = xt.shape
+    width = chans // 2
+    mine = pl.ds(pl.multiple_of(c * width, 8), width)
     nb = chans // T
     share = len(lower) // 2
     rows = share * T
@@ -116,7 +117,7 @@
     order = [lax.rem(r + d, n) for d in range(1, n)] + [r]
     loads = []
     for i, b in enumerate(order):
-        cp = pltpu.make_async_copy(x_hbm.at[b, pl.ds(pl.multiple_of(c * half, T), half), :], own.at[b], lsem.at[i])
+        cp = pltpu.make_async_copy(x_hbm.at[b, :, pl.ds(pl.multiple_of(c * half, T), half)], xt.at[b, mine, :], lsem.at[i])
         cp.start()
         loads.append(cp)
     pl.semaphore_wait(barrier, n)
@@ -127,7 +128,7 @@
         cp.start()
         return cp
 
-    swaps = [remote(x_hbm.at[b, pl.ds(pl.multiple_of(other * half, T), half), :], got.at[b],
+    swaps = [remote(x_hbm.at[b, :, pl.ds(pl.multiple_of(other * half, T), half)], xt.at[b, mine, :],
                     xs.at[i], xr.at[i], {"chn": other}) for i, b in enumerate(order)]
 
     sends = []
@@ -137,7 +138,7 @@
         swap.wait()
         for s in range(share):
             part[b, s * T:(s + 1) * T, :] = gram[b, c * share + s] + gram_rx[b, s]
-        count = jnp.sum(mask_ref[b].astype(jnp.float32))
+        count = jnp.sum(mask_ref[pl.ds(b, 1), :].astype(jnp.float32))
         part[b, rows:rows + 8, :] = jnp.full((8, T), count, jnp.float32)
         if i < n - 1:
             sends.append(remote(part.at[b], rs_rx.at[i], rss.at[i], rsr.at[i], {"rng": b}))
@@ -146,11 +147,7 @@
     for i, b in enumerate(order):
         loads[i].wait()
         swaps[i].wait()
-        mine, theirs = own[b], got[b]
-        first = c == 0
-        xt[b, :width, :] = jnp.where(first, mine, theirs).T
-        xt[b, width:, :] = jnp.where(first, theirs, mine).T
-        mask = mask_ref[b, :, pl.ds(pl.multiple_of(c * half, T), half)].astype(jnp.bfloat16)
+        mask = mask_ref[pl.ds(b, 1), pl.ds(pl.multiple_of(c * half, T), half)].astype(jnp.bfloat16)
         xb = xt[b]
         g = lax.dot_general(xb * mask, xb, (((1,), (1,)), ((), ())), preferred_element_type=jnp.float32)
         for s, (p, q) in enumerate(lower):
@@ -247,8 +244,6 @@
         in_specs=[pl.BlockSpec(memory_space=pl.ANY), vmem, vmem],
         out_specs=(vmem, vmem),
         scratch_shapes=[
-            pltpu.VMEM((bins, half, width), bf16),
-            pltpu.VMEM((bins, half, width), bf16),
             pltpu.VMEM((bins, chans, half), bf16),
             pltpu.VMEM((bins, len(lower), T, T), f32),
             pltpu.VMEM((bins, share, T, T), f32),
@@ -266,7 +261,7 @@
             sem((n - 1,)), sem((n - 1,)), sem((n - 1,)), sem((n - 1,)),
         ],
         compiler_params=pltpu.CompilerParams(collective_id=0, has_side_effects=True, vmem_limit_bytes=56 * 2**20),
-    )(samples, train_mask[:, None, :], steer)
+    )(jnp.swapaxes(samples, 1, 2), train_mask, steer)
     return amf, power[:, 0, :]
 
 

time: 80.6 us -> 72.2 us (0.90)
  local copies, waits for them, and re-layouts: 10.4 us -> 3 us
    unnamed x3 -> x2, local copies, waits for them, and re-layouts: 8.98 us -> 3 us
    broadcast_in_dim x1 -> x0, local copies, waits for them, and re-layouts: 1.39 us -> none  [fused_body(): train_mask[:, None, :]]
where the time goes in v2:
time: 72.2 us; the launch traced here: 72 us
  Pallas kernels  66.8 us (93%)
  local copies, waits for them, and re-layouts  3 us (4%)
  other arithmetic  1.53 us (2%)
    pallas_call x1, Pallas kernels, fused_body(): pl.pallas_call(functools.partial(kernel, n, lower), name='amf', out_shape...  66.8 us
    unnamed x2, local copies, waits for them, and re-layouts  3 us

profile of v2, /device:TPU:24, one launch (start us, length us, event | category | flops | bytes accessed | tf_op | source)
XLA Modules:
  0.0 72.0 jit_solution(15952209956309748945)
XLA Ops:
  0.6 0.7 sine_multiply_fusion
  1.3 0.1 multiply_cosine_fusion
  1.5 0.7 maximum_bitcast_fusion.steer_ref
  2.2 66.8 %amf.1 = (f32[4,16,1024]{2,1,0:T(8,128)}, f32[4,1,1024]{2,1,0:T(1,128)}) custom-call(bf16[4,192,2048]{2,1,0:T(8,128)(2,1)} %bitcast.6, s32[4,2048]{1,0:T(4,128)} %mask_ref.1, f32[16,384]{1,0:T(8,128)} %maximum_bitcast_fusion.steer_ref), custom_call_target="tpu_custom_call" | custom-call | tf_op jit(solution)/shard_map/amf/pallas_call | solution.py:239
  69.0 1.3 %copy.7 = f32[4,1,1024]{2,0,1:T(4,128)} copy(f32[4,1,1024]{2,1,0:T(1,128)} %get-tuple-element.5) | data formatting | bytes 32768
  70.3 1.7 %copy.9 = f32[4,16,1024]{2,1,0:T(8,128)} copy(f32[4,16,1024]{2,1,0:T(8,128)} %get-tuple-element.10) | data formatting | bytes 524288
  (1 shorter events, 0.0 us)
